TPU v7x, 32 devices: a whole 2x2x4 slice. The times are simulated.
32 devices in a mesh: sims: 2 (over x), rows: 4 (over y, core), fields: 4 (over z).
Axes of the slice: x: 2, y: 2, z: 4, core: 2. Of those that a mesh axis runs over, the one named last changes fastest.
Arguments:
- sky_maps: float32 [6, 32, 16384], P('sims', 'rows', 'fields'), parts along dimension 0, may hold values from -7 to 7
- band_cuts: int32 [6], replicated, may hold values from 1 to 8191, as said below
- filters: float32 [3, 32, 16384], P(None, ('rows', 'fields')), may hold values from 0.3 to 3
- wiener: float32 [2, 32, 16384], P(None, ('rows', 'fields')), may hold values from 0.3 to 3
- response: float32 [32, 16384], P(('rows', 'fields')), may hold values from 0.5 to 2
Outputs:
- phi_curl: float32 [4, 32, 16384], P('sims', 'rows', 'fields'), parts along dimension 0
There are 2 independent parts, one for each index of `sims`. A program takes and returns all parts, laid end to end along the dimension named above; an argument that names none is the same for every part. Nothing has to cross between parts.
Inputs may be any that keep to these rules, and one draw needn't show every extreme that they name: `band_cuts`: entries 0, 2 and 4 are the smallest multipole indices of the temperature, polarization and estimate bands and lie below 512; entries 1, 3 and 5 are the largest and are at least 4096.
All inputs are finite; a program needn't handle non-finite values.
Results may differ from a plain program's by a relative error of at most 0.00019.
Values sent between devices are 32-bit elements; how exact they have to be, the bound alone decides.
No kernel may reach another device: no remote copies, remote signals or barrier semaphores. Data moves between devices by JAX's collectives and lax.ppermute only.
A program may use at most 128 MiB of HBM per device.

v0:
```python
import math
import jax
import jax.numpy as jnp
from jax import lax
from jax.sharding import PartitionSpec as P

NC = 16384
exact_mode = lax.Precision.HIGHEST


def split_factor(length):
    best_first = 1
    for divisor in range(1, math.isqrt(length) + 1):
        if length % divisor == 0:
            best_first = divisor
    return (best_first, length // best_first)


def phase_table(left_index, right_index, period, direction):
    product = left_index[:, None] * right_index[None, :] % period
    angles = direction * 2.0 * math.pi / period * product.astype(jnp.float32)
    return (jnp.cos(angles), jnp.sin(angles))


def complex_einsum(formula, data_pair, table_pair):
    data_real, data_imag = data_pair
    table_real, table_imag = table_pair
    real_out = jnp.einsum(formula, data_real, table_real, precision=exact_mode)
    imag_out = jnp.einsum(formula, data_real, table_imag, precision=exact_mode)
    if data_imag is not None:
        real_out = real_out - jnp.einsum(formula, data_imag, table_imag, precision=exact_mode)
        imag_out = imag_out + jnp.einsum(formula, data_imag, table_real, precision=exact_mode)
    return (real_out, imag_out)


def complex_mul(left_pair, right_pair):
    return (
        left_pair[0] * right_pair[0] - left_pair[1] * right_pair[1],
        left_pair[0] * right_pair[1] + left_pair[1] * right_pair[0],
    )


def conj_mul(left_pair, right_pair):
    return (
        left_pair[0] * right_pair[0] + left_pair[1] * right_pair[1],
        left_pair[0] * right_pair[1] - left_pair[1] * right_pair[0],
    )


def row_transform(data_pair, direction):
    batch_len, length, block_width = data_pair[0].shape
    outer_len, inner_len = split_factor(length)
    outer_ids = jnp.arange(outer_len, dtype=jnp.int32)
    inner_ids = jnp.arange(inner_len, dtype=jnp.int32)
    real_in = data_pair[0].reshape(batch_len, outer_len, inner_len, block_width)
    imag_in = None
    if data_pair[1] is not None:
        imag_in = data_pair[1].reshape(batch_len, outer_len, inner_len, block_width)
    middle = complex_einsum(
        "bjmc,jk->bkmc", (real_in, imag_in), phase_table(outer_ids, outer_ids, outer_len, direction)
    )
    twiddle = phase_table(outer_ids, inner_ids, length, direction)
    middle = complex_mul(middle, (twiddle[0][None, :, :, None], twiddle[1][None, :, :, None]))
    result = complex_einsum(
        "bkmc,mq->bqkc", middle, phase_table(inner_ids, inner_ids, inner_len, direction)
    )
    norm_factor = 1.0 if direction < 0 else 1.0 / length
    return (
        result[0].reshape(batch_len, length, block_width) * norm_factor,
        result[1].reshape(batch_len, length, block_width) * norm_factor,
    )


def block_order(groups, fields_count):
    positions = jnp.arange(groups, dtype=jnp.int32)
    blocks = positions % fields_count * (groups // fields_count) + positions // fields_count
    return (positions, blocks)


def column_forward(data_pair, groups, fields_count):
    batch_len, local_rows, total_len = data_pair[0].shape
    block_width = total_len // groups
    positions, blocks = block_order(groups, fields_count)
    column_ids = jnp.arange(block_width, dtype=jnp.int32)
    shaped = (
        data_pair[0].reshape(batch_len, local_rows, groups, block_width),
        data_pair[1].reshape(batch_len, local_rows, groups, block_width),
    )
    middle = complex_einsum("brpc,pk->brkc", shaped, phase_table(blocks, positions, groups, -1.0))
    twiddle = phase_table(positions, column_ids, total_len, -1.0)
    middle = complex_mul(middle, (twiddle[0][None, None], twiddle[1][None, None]))
    result = complex_einsum(
        "brkc,cq->brqk", middle, phase_table(column_ids, column_ids, block_width, -1.0)
    )
    return (
        result[0].reshape(batch_len, local_rows, total_len),
        result[1].reshape(batch_len, local_rows, total_len),
    )


def column_inverse(data_pair, groups, fields_count):
    batch_len, local_rows, total_len = data_pair[0].shape
    block_width = total_len // groups
    positions, blocks = block_order(groups, fields_count)
    column_ids = jnp.arange(block_width, dtype=jnp.int32)
    shaped = (
        data_pair[0].reshape(batch_len, local_rows, block_width, groups),
        data_pair[1].reshape(batch_len, local_rows, block_width, groups),
    )
    middle = complex_einsum(
        "brqk,qc->brkc", shaped, phase_table(column_ids, column_ids, block_width, 1.0)
    )
    twiddle = phase_table(positions, column_ids, total_len, 1.0)
    middle = complex_mul(middle, (twiddle[0][None, None], twiddle[1][None, None]))
    result = complex_einsum("brkc,kp->brpc", middle, phase_table(positions, blocks, groups, 1.0))
    norm_factor = 1.0 / total_len
    return (
        result[0].reshape(batch_len, local_rows, total_len) * norm_factor,
        result[1].reshape(batch_len, local_rows, total_len) * norm_factor,
    )


def body(sky_maps, band_cuts, filters, wiener, response):
    rows_count = lax.axis_size("rows")
    fields_count = lax.axis_size("fields")
    groups = rows_count * fields_count
    local_rows = filters.shape[1]
    total_rows = local_rows * groups
    row_ratio = NC // total_rows

    def forward_columns(stacked):
        return jnp.stack(column_forward((stacked[0], stacked[1]), groups, fields_count))

    def inverse_rows(stacked):
        return jnp.stack(row_transform((stacked[0], stacked[1]), 1.0))

    def inverse_columns(stacked):
        return jnp.stack(column_inverse((stacked[0], stacked[1]), groups, fields_count))

    def to_frequency(stacked):
        batch_len = stacked.shape[1]
        block_width = stacked.shape[3]
        shaped = stacked.reshape(
            2, batch_len, rows_count, fields_count, local_rows, 1, 1, block_width
        )
        arrived = lax.all_to_all(
            lax.all_to_all(shaped, "rows", split_axis=2, concat_axis=5, tiled=True),
            "fields",
            split_axis=3,
            concat_axis=6,
            tiled=True,
        )
        result = forward_columns(arrived.reshape(2, batch_len, local_rows, groups * block_width))
        return result

    def to_space(stacked):
        batch_len = stacked.shape[1]
        block_width = stacked.shape[3] // groups
        shaped = stacked.reshape(
            2, batch_len, 1, 1, local_rows, rows_count, fields_count, block_width
        )
        arrived = lax.all_to_all(
            lax.all_to_all(shaped, "rows", split_axis=5, concat_axis=2, tiled=True),
            "fields",
            split_axis=6,
            concat_axis=3,
            tiled=True,
        )
        result = inverse_rows(arrived.reshape(2, batch_len, total_rows, block_width))
        return result

    slab_spectra = jnp.stack(
        row_transform(
            (lax.all_to_all(sky_maps, "rows", split_axis=2, concat_axis=1, tiled=True), None), -1.0
        )
    )
    sky_spectra = to_frequency(slab_spectra)
    row_ids = lax.axis_index(("rows", "fields")) * local_rows + jnp.arange(
        local_rows, dtype=jnp.int32
    )
    freq_rows = jnp.where(row_ids < total_rows // 2, row_ids, row_ids - total_rows)[:, None]
    column_ids = jnp.arange(NC, dtype=jnp.int32)
    freq_cols = jnp.where(column_ids < NC // 2, column_ids, column_ids - NC)[None, :]
    scaled_rows = row_ratio * freq_rows
    radius_sq = freq_cols * freq_cols + scaled_rows * scaled_rows

    def band_mask(lower_cut, upper_cut):
        inside = (radius_sq >= lower_cut * lower_cut) & (radius_sq <= upper_cut * upper_cut)
        return inside.astype(jnp.float32)

    mask_temp = band_mask(band_cuts[0], band_cuts[1])
    mask_pol = band_mask(band_cuts[2], band_cuts[3])
    mask_out = band_mask(band_cuts[4], band_cuts[5])
    radius_floor = jnp.maximum(radius_sq, 1).astype(jnp.float32)
    cos_two = (freq_cols * freq_cols - scaled_rows * scaled_rows).astype(jnp.float32) / radius_floor
    sin_two = (2 * freq_cols * scaled_rows).astype(jnp.float32) / radius_floor
    along_x = (2 * freq_cols).astype(jnp.float32) / NC
    along_y = (2 * freq_rows).astype(jnp.float32) / total_rows
    raising = (-along_y + 0.0 * along_x, along_x + 0.0 * along_y)
    lowering = (along_y + 0.0 * along_x, along_x + 0.0 * along_y)
    rotation = (cos_two, sin_two)
    temp_modes = (sky_spectra[0, 0], sky_spectra[1, 0])
    stokes_q = (sky_spectra[0, 1], sky_spectra[1, 1])
    stokes_u = (sky_spectra[0, 2], sky_spectra[1, 2])
    e_modes = (
        -(cos_two * stokes_q[0] + sin_two * stokes_u[0]),
        -(cos_two * stokes_q[1] + sin_two * stokes_u[1]),
    )
    b_modes = (
        sin_two * stokes_q[0] - cos_two * stokes_u[0],
        sin_two * stokes_q[1] - cos_two * stokes_u[1],
    )
    temp_weight = mask_temp * filters[0]
    e_weight = mask_pol * filters[1]
    b_weight = mask_pol * filters[2]
    temp_bar = (temp_weight * temp_modes[0], temp_weight * temp_modes[1])
    e_bar = (e_weight * e_modes[0], e_weight * e_modes[1])
    b_bar = (b_weight * b_modes[0], b_weight * b_modes[1])
    grad_temp = complex_mul(raising, (wiener[0] * temp_bar[0], wiener[0] * temp_bar[1]))
    pol_sum = complex_mul((e_bar[0] - b_bar[1], e_bar[1] + b_bar[0]), rotation)
    pol_bar = (-pol_sum[0], -pol_sum[1])
    pol_rot = complex_mul((wiener[1] * e_bar[0], wiener[1] * e_bar[1]), rotation)
    pol_wiener = (-pol_rot[0], -pol_rot[1])
    spin_three = complex_mul(raising, pol_wiener)
    spin_one = complex_mul(lowering, pol_wiener)
    leg_spectra = jnp.stack(
        [
            jnp.stack([temp_bar[0], grad_temp[0], pol_bar[0], spin_three[0], spin_one[0]]),
            jnp.stack([temp_bar[1], grad_temp[1], pol_bar[1], spin_three[1], spin_one[1]]),
        ]
    )
    leg_maps = to_space(inverse_columns(leg_spectra))
    temp_leg = (leg_maps[0, 0], leg_maps[1, 0])
    grad_leg = (leg_maps[0, 1], leg_maps[1, 1])
    pol_leg = (leg_maps[0, 2], leg_maps[1, 2])
    three_leg = (leg_maps[0, 3], leg_maps[1, 3])
    one_leg = (leg_maps[0, 4], leg_maps[1, 4])
    temp_term = complex_mul(temp_leg, grad_leg)
    raise_term = conj_mul(pol_leg, three_leg)
    lower_term = conj_mul(one_leg, pol_leg)
    current = (
        temp_term[0] + 0.5 * (raise_term[0] + lower_term[0]),
        temp_term[1] + 0.5 * (raise_term[1] + lower_term[1]),
    )
    current_rows = jnp.stack(row_transform((current[0][None], current[1][None]), -1.0))
    current_modes = to_frequency(current_rows)
    out_weight = mask_out * response
    estimate_modes = complex_mul(
        lowering, (out_weight * current_modes[0, 0], out_weight * current_modes[1, 0])
    )
    estimate_stack = jnp.stack([estimate_modes[0][None], estimate_modes[1][None]])
    estimate_maps = to_space(inverse_columns(estimate_stack))
    slab_result = estimate_maps[:, 0]
    return lax.all_to_all(slab_result, "rows", split_axis=1, concat_axis=2, tiled=True)


def solution(mesh):
    placed = (
        P("sims", "rows", "fields"),
        P(),
        P(None, ("rows", "fields"), None),
        P(None, ("rows", "fields"), None),
        P(("rows", "fields"), None),
    )
    return jax.shard_map(
        body, mesh=mesh, in_specs=placed, out_specs=P("sims", "rows", "fields"), check_vma=False
    )
```

profile of v0, /device:TPU:0, one launch (start us, length us, event | category | flops | bytes accessed | tf_op | source)
XLA Modules:
  0.0 572.1 jit_solution(2138556085943826780)
XLA Ops:
  0.0 6.7 %copy.84 = f32[3,8,4096]{1,0,2:T(4,128)} copy(f32[3,8,4096]{2,1,0:T(8,128)} %param.5) | data formatting | bytes 786432 | tf_op args[0]
  6.7 7.5 %reshape.1834 = f32[4,1,24576]{2,1,0:T(1,128)} reshape(f32[4096,3,8]{2,1,0:T(4,128)} %bitcast.453) | data formatting | bytes 786432
  14.2 4.3 all-to-all-start
  18.5 7.4 %all-to-all-done = f32[4,1,24576]{2,1,0:T(1,128)S(1)} async-done(((f32[4,1,24576]{2,1,0:T(1,128)}), f32[4,1,24576]{2,1,0:T(1,128)S(1)}, u32[]{:S(2)}, u32[]{:S(2)}) %all-to-all-start) | async-done | bytes 393248 | tf_op jit(solution)/shard_map/all_to_all | solution.py:174
  26.4 1.8 reduce
  28.1 8.7 %reshape.1835 = f32[4096,3,8]{2,1,0:T(4,128)} reshape(f32[4,24576]{1,0:T(4,128)S(1)} %reduce) | data formatting | bytes 786432
  36.9 6.9 %copy.170 = f32[3,8,4,1024]{3,2,1,0:T(4,128)S(1)} copy(f32[3,8,4,1024]{1,0,3,2:T(4,128)} %bitcast.452) | data formatting | bytes 786432 | tf_op jit(solution)/shard_map/all_to_all | solution.py:174
  43.8 0.8 fusion.133
  44.7 0.9 add_bitcast_fusion.1
  50.1 14.0 %all_to_all.165 = f32[2,3,4,4,2,1,1,1024]{7,4,3,1,6,5,0,2:T(2,128)S(1)} all-to-all(f32[2,3,4,4,2,1,1,1024]{7,4,3,1,6,5,0,2:T(2,128)S(1)} %copy.92), channel_id=1, replica_groups=mesh['sims'=2,'rows'=4,'fields'=4] {'rows'}, dimensions={2} | all-to-all | bytes 1572864 | tf_op jit(solution)/shard_map/all_to_all | solution.py:147
  64.1 1.0 copy.93
  65.1 5.7 all-to-all-start.2
  78.8 11.8 %all-to-all-done.2 = f32[2,3,1,4,2,4,1,1024]{7,4,5,1,0,6,2,3:T(2,128)S(1)} async-done(((f32[2,3,1,4,2,4,1,1024]{7,4,5,1,0,6,2,3:T(2,128)}), f32[2,3,1,4,2,4,1,1024]{7,4,5,1,0,6,2,3:T(2,128)S(1)}, u32[]{:S(2)}, u32[]{:S(2)}) %all-to-all-start.2) | async-done | bytes 786464 | tf_op jit(solution)/shard_map/all_to_all | solution.py:146
  93.6 18.6 %fusion.24 = f32[1024,3,2,16]{0,3,2,1:T(8,128)S(1)} fusion(f32[16,3,2,1024]{3,0,2,1:T(8,128)S(1)} %convolution_add_fusion.3, f32[16,3,2,1024]{3,0,2,1:T(8,128)S(1)} %convolution_subtract_fusion.3, f32[16,1024]{1,0:T(8,128)S(1)} %get-tuple-element.50, f32[16,1024]{1,0:T(8,128)S(1)} %get-tuple-element.51), kind=kOutput, calls=%fused_computation.27 | convolution fusion | flops 1222934528 | bytes 1310720 | tf_op jit(solution)/shard_map/brkc,cq->brqk/dot_general | solution.py:28
  112.1 19.3 %fusion.22 = f32[1024,3,2,16]{0,3,2,1:T(8,128)} fusion(f32[16,3,2,1024]{3,0,2,1:T(8,128)S(1)} %convolution_add_fusion.3, f32[16,3,2,1024]{3,0,2,1:T(8,128)S(1)} %convolution_subtract_fusion.3, f32[16,1024]{1,0:T(8,128)S(1)} %get-tuple-element.50, f32[16,1024]{1,0:T(8,128)S(1)} %get-tuple-element.51), kind=kOutput, calls=%fused_computation.25 | convolution fusion | flops 1222934528 | bytes 1310720 | tf_op jit(solution)/shard_map/brkc,cq->brqk/dot_general | solution.py:32
  131.4 19.2 %fusion.88 = f32[3,2,1024,16]{2,3,1,0:T(8,128)} fusion(f32[1024,3,2,16]{0,3,2,1:T(8,128)S(1)} %fusion.24, f32[16,3,2,1024]{3,0,2,1:T(8,128)S(1)} %convolution_add_fusion.3, f32[16,3,2,1024]{3,0,2,1:T(8,128)S(1)} %convolution_subtract_fusion.3, f32[16,1024]{1,0:T(8,128)S(1)} %get-tuple-element.50, f32[16,1024]{1,0:T(8,128)S(1)} %get-tuple-element.51), kind=kOutput, calls=%fused_computation.84 | convolution fusion | flops 1223032832 | bytes 1703936 | tf_op jit(solution)/shard_map/brkc,cq->brqk/dot_general | solution.py:31
  150.6 1.9 copy.96
  152.5 2.5 stack_reshape.4
  155.0 20.8 %fusion.94 = f32[3,2,1024,16]{2,3,1,0:T(8,128)} fusion(f32[1024,3,2,16]{0,3,2,1:T(8,128)} %fusion.22, f32[16,3,2,1024]{3,0,2,1:T(8,128)} %copy-done.6, f32[16,3,2,1024]{3,0,2,1:T(8,128)} %copy-done.5, f32[16,1024]{1,0:T(8,128)} %copy-done.8, f32[16,1024]{1,0:T(8,128)} %copy-done.10), kind=kOutput, calls=%fused_computation.86 | convolution fusion | flops 1223032832 | bytes 1703936 | tf_op jit(solution)/shard_map/brkc,cq->brqk/dot_general | solution.py:29
  175.9 1.9 copy.97
  177.8 2.4 stack_reshape.5
  180.2 2.9 fusion.150
  183.1 1.3 fusion.152
  186.5 1.5 subtract_negate_fusion.1
  189.1 1.3 fusion.153
  191.2 1.3 stack.74
  195.4 20.3 %fusion.16 = f32[5,2,16,1024]{3,2,1,0:T(8,128)} fusion(f32[5,2,1024,16]{2,3,1,0:T(8,128)} %constant_dynamic-update-slice_fusion), kind=kOutput, calls=%fused_computation.19 | convolution fusion | flops 2027945984 | bytes 1310720 | tf_op jit(solution)/shard_map/brqk,qc->brkc/dot_general | solution.py:28
  218.9 0.8 copy-done.13
  219.8 18.7 %fusion.14 = f32[5,2,16,1024]{3,2,1,0:T(8,128)S(1)} fusion(f32[5,2,1024,16]{2,3,1,0:T(8,128)S(1)} %constant_dynamic-update-slice_fusion.5), kind=kOutput, calls=%fused_computation.17 | convolution fusion | flops 2027945984 | bytes 1310720 | tf_op jit(solution)/shard_map/brqk,qc->brkc/dot_general | solution.py:32
  238.5 20.2 %fusion.77 = f32[5,2,16,1024]{3,2,1,0:T(8,128)S(1)} fusion(f32[5,2,16,1024]{3,2,1,0:T(8,128)S(1)} %copy-done.19, f32[5,2,1024,16]{2,3,1,0:T(8,128)} %copy-done.13), kind=kOutput, calls=%fused_computation.75 | convolution fusion | flops 2028109824 | bytes 1966080 | tf_op jit(solution)/shard_map/brqk,qc->brkc/dot_general | solution.py:31
  258.8 18.8 %fusion.80 = f32[5,2,16,1024]{3,2,1,0:T(8,128)S(1)} fusion(f32[5,2,16,1024]{3,2,1,0:T(8,128)S(1)} %fusion.14, f32[5,2,1024,16]{2,3,1,0:T(8,128)S(1)} %copy-done.12), kind=kOutput, calls=%fused_computation.76 | convolution fusion | flops 2028109824 | bytes 1966080 | tf_op jit(solution)/shard_map/brqk,qc->brkc/dot_general | solution.py:29
  277.5 0.8 fusion.147
  278.3 0.8 fusion.146
  279.1 0.8 fusion.70
  280.1 0.8 fusion.72
  281.6 19.7 %all_to_all.166 = f32[2,5,1,1,2,4,4,1024]{7,6,4,1,3,2,0,5:T(4,128)S(1)} all-to-all(f32[2,5,1,1,2,4,4,1024]{7,6,4,1,3,2,0,5:T(4,128)S(1)} %copy.171), channel_id=1, replica_groups=mesh['sims'=2,'rows'=4,'fields'=4] {'rows'}, dimensions={5} | all-to-all | bytes 2621440 | tf_op jit(solution)/shard_map/all_to_all | solution.py:163
  301.3 2.0 copy.110
  303.2 3.7 all-to-all-start.4
  307.0 31.0 %all-to-all-done.4 = f32[2,5,4,1,2,1,4,1024]{7,2,4,1,0,5,3,6:T(4,128)S(1)} async-done(((f32[2,5,4,1,2,1,4,1024]{7,2,4,1,0,5,3,6:T(4,128)}), f32[2,5,4,1,2,1,4,1024]{7,2,4,1,0,5,3,6:T(4,128)S(1)}, u32[]{:S(2)}, u32[]{:S(2)}) %all-to-all-start.4) | async-done | bytes 1310752 | tf_op jit(solution)/shard_map/all_to_all | solution.py:162
  338.2 1.2 fusion.282
  339.4 1.2 fusion.280
  340.7 1.3 convolution_add_fusion.2
  342.0 1.5 add_bitcast_fusion
  343.5 1.0 fusion.127
  344.5 1.0 fusion.125
  345.5 1.0 fusion.74
  347.2 1.0 fusion.76
  349.9 0.8 convolution_subtract_fusion.10
  353.2 8.4 %all_to_all.167 = f32[2,1,4,4,2,1,1,1024]{7,4,3,6,5,1,0,2:T(2,128)S(1)} all-to-all(f32[2,1,4,4,2,1,1,1024]{7,4,3,6,5,1,0,2:T(2,128)S(1)} %copy.129), channel_id=1, replica_groups=mesh['sims'=2,'rows'=4,'fields'=4] {'rows'}, dimensions={2} | all-to-all | bytes 524288 | tf_op jit(solution)/shard_map/all_to_all | solution.py:147
  361.6 0.7 copy.130
  362.3 3.4 all-to-all-start.6
  368.1 6.4 %all-to-all-done.6 = f32[2,1,1,4,2,4,1,1024]{7,4,5,0,6,2,1,3:T(2,128)S(1)} async-done(((f32[2,1,1,4,2,4,1,1024]{7,4,5,0,6,2,1,3:T(2,128)}), f32[2,1,1,4,2,4,1,1024]{7,4,5,0,6,2,1,3:T(2,128)S(1)}, u32[]{:S(2)}, u32[]{:S(2)}) %all-to-all-start.6) | async-done | bytes 262176 | tf_op jit(solution)/shard_map/all_to_all | solution.py:146
  376.1 18.3 %fusion.12 = f32[1024,2,16]{0,2,1:T(8,128)S(1)} fusion(f32[16,1,2,1024]{3,0,2,1:T(8,128)S(1)} %fusion.97, f32[16,1,2,1024]{3,0,2,1:T(8,128)S(1)} %fusion.98, f32[16,1024]{1,0:T(8,128)S(1)} %copy-done.9, f32[16,1024]{1,0:T(8,128)S(1)} %copy-done.11), kind=kOutput, calls=%fused_computation.15 | convolution fusion | flops 417431552 | bytes 524288 | tf_op jit(solution)/shard_map/brkc,cq->brqk/dot_general | solution.py:31
  394.4 18.3 %fusion.10 = f32[1024,2,16]{0,2,1:T(8,128)S(1)} fusion(f32[16,1,2,1024]{3,0,2,1:T(8,128)S(1)} %fusion.97, f32[16,1,2,1024]{3,0,2,1:T(8,128)S(1)} %fusion.98, f32[16,1024]{1,0:T(8,128)S(1)} %copy-done.9, f32[16,1024]{1,0:T(8,128)S(1)} %copy-done.11), kind=kOutput, calls=%fused_computation.13 | convolution fusion | flops 417431552 | bytes 524288 | tf_op jit(solution)/shard_map/brkc,cq->brqk/dot_general | solution.py:29
  412.8 18.4 %fusion.114 = f32[1,2,1024,16]{2,3,1,0:T(8,128)S(1)} fusion(f32[1024,2,16]{0,2,1:T(8,128)S(1)} %fusion.12, f32[16,1,2,1024]{3,0,2,1:T(8,128)S(1)} %fusion.97, f32[16,1,2,1024]{3,0,2,1:T(8,128)S(1)} %fusion.98, f32[16,1024]{1,0:T(8,128)S(1)} %copy-done.9, f32[16,1024]{1,0:T(8,128)S(1)} %copy-done.11), kind=kOutput, calls=%fused_computation.110 | convolution fusion | flops 417464320 | bytes 655360 | tf_op jit(solution)/shard_map/brkc,cq->brqk/dot_general | solution.py:28
  432.1 18.2 %fusion.120 = f32[1,2,1024,16]{2,3,1,0:T(8,128)S(1)} fusion(f32[1024,2,16]{0,2,1:T(8,128)S(1)} %fusion.10, f32[16,1,2,1024]{3,0,2,1:T(8,128)S(1)} %fusion.97, f32[16,1,2,1024]{3,0,2,1:T(8,128)S(1)} %fusion.98, f32[16,1024]{1,0:T(8,128)S(1)} %copy-done.9, f32[16,1024]{1,0:T(8,128)S(1)} %copy-done.11), kind=kOutput, calls=%fused_computation.112 | convolution fusion | flops 417464320 | bytes 655360 | tf_op jit(solution)/shard_map/brkc,cq->brqk/dot_general | solution.py:32
  452.0 21.4 %fusion.4 = f32[2,16,1024]{2,1,0:T(8,128)S(1)} fusion(f32[2,1024,16]{2,1,0:T(8,128)S(1)} %reshape.1797), kind=kOutput, calls=%fused_computation.7 | convolution fusion | flops 417333248 | bytes 262144 | tf_op jit(solution)/shard_map/brqk,qc->brkc/dot_general | solution.py:31
  473.8 21.2 %fusion.2 = f32[2,16,1024]{2,1,0:T(8,128)S(1)} fusion(f32[2,1024,16]{2,1,0:T(8,128)S(1)} %reshape.1796), kind=kOutput, calls=%fused_computation.5 | convolution fusion | flops 417333248 | bytes 262144 | tf_op jit(solution)/shard_map/brqk,qc->brkc/dot_general | solution.py:29
  494.9 21.5 %fusion.105 = f32[2,16,1024]{2,1,0:T(8,128)S(1)} fusion(f32[2,16,1024]{2,1,0:T(8,128)S(1)} %fusion.4, f32[2,1024,16]{2,1,0:T(8,128)S(1)} %reshape.1796), kind=kOutput, calls=%fused_computation.107 | convolution fusion | flops 417366016 | bytes 393216 | tf_op jit(solution)/shard_map/brqk,qc->brkc/dot_general | solution.py:28
  516.4 21.1 %fusion.108 = f32[2,16,1024]{2,1,0:T(8,128)S(1)} fusion(f32[2,16,1024]{2,1,0:T(8,128)S(1)} %fusion.2, f32[2,1024,16]{2,1,0:T(8,128)S(1)} %reshape.1797), kind=kOutput, calls=%fused_computation.108 | convolution fusion | flops 417366016 | bytes 393216 | tf_op jit(solution)/shard_map/brqk,qc->brkc/dot_general | solution.py:32
  539.2 8.4 %all_to_all.168 = f32[2,1,1,1,2,4,4,1024]{7,6,4,3,2,1,0,5:T(4,128)S(1)} all-to-all(f32[2,1,1,1,2,4,4,1024]{7,6,4,3,2,1,0,5:T(4,128)S(1)} %copy.172), channel_id=1, replica_groups=mesh['sims'=2,'rows'=4,'fields'=4] {'rows'}, dimensions={5} | all-to-all | bytes 524288 | tf_op jit(solution)/shard_map/all_to_all | solution.py:163
  547.7 11.3 %all_to_all.169 = f32[2,1,4,1,2,1,4,1024]{7,2,4,0,5,3,1,6:T(4,128)S(1)} all-to-all(f32[2,1,4,1,2,1,4,1024]{7,2,4,0,5,3,1,6:T(4,128)S(1)} %copy.141), channel_id=1, replica_groups=mesh['sims'=2,'rows'=4,'fields'=4] {'fields'}, dimensions={6} | all-to-all | bytes 524288 | tf_op jit(solution)/shard_map/all_to_all | solution.py:162
  562.7 8.4 %all_to_all.170 = f32[2,32,1024]{2,0,1:T(2,128)S(1)} all-to-all(f32[2,32,1024]{2,0,1:T(2,128)S(1)} %copy.148), channel_id=1, replica_groups=mesh['sims'=2,'rows'=4,'fields'=4] {'rows'}, dimensions={1} | all-to-all | bytes 524288 | tf_op jit(solution)/shard_map/all_to_all | solution.py:254
  571.1 0.8 copy.149
  (165 shorter events, 36.2 us)
Async XLA Ops:
  14.2 11.7 %all-to-all-start = ((f32[4,1,24576]{2,1,0:T(1,128)}), f32[4,1,24576]{2,1,0:T(1,128)S(1)}, u32[]{:S(2)}, u32[]{:S(2)}) async-start(f32[4,1,24576]{2,1,0:T(1,128)} %reshape.1834), calls=%async_computation | async-start | bytes 786432 | tf_op jit(solution)/shard_map/all_to_all | solution.py:174
  49.1 21.7 %copy-start.14 = (s32[6]{0:T(128)S(1)}, s32[6]{0:T(128)}, u32[]{:S(2)}) copy-start(s32[6]{0:T(128)} %param.6) | copy-start | bytes 76
  65.1 25.4 %all-to-all-start.2 = ((f32[2,3,1,4,2,4,1,1024]{7,4,5,1,0,6,2,3:T(2,128)}), f32[2,3,1,4,2,4,1,1024]{7,4,5,1,0,6,2,3:T(2,128)S(1)}, u32[]{:S(2)}, u32[]{:S(2)}) async-start(f32[2,3,1,4,2,4,1,1024]{7,4,5,1,0,6,2,3:T(2,128)} %copy.93), calls=%async_computation.2 | async-start | bytes 1572864 | tf_op jit(solution)/shard_map/all_to_all | solution.py:146
  78.4 53.0 %copy-start.8 = (f32[16,1024]{1,0:T(8,128)}, f32[16,1024]{1,0:T(8,128)S(1)}, u32[]{:S(2)}) copy-start(f32[16,1024]{1,0:T(8,128)S(1)} %get-tuple-element.50) | copy-start | bytes 196612
  78.4 53.0 %copy-start.10 = (f32[16,1024]{1,0:T(8,128)}, f32[16,1024]{1,0:T(8,128)S(1)}, u32[]{:S(2)}) copy-start(f32[16,1024]{1,0:T(8,128)S(1)} %get-tuple-element.51) | copy-start | bytes 196612
  78.7 107.7 %copy-start.2 = (s32[16384]{0:T(1024)}, s32[16384]{0:T(1024)S(1)}, u32[]{:S(2)}) copy-start(s32[16384]{0:T(1024)S(1)} %get-tuple-element.54) | copy-start | bytes 196612
  93.0 38.4 %copy-start.5 = (f32[16,3,2,1024]{3,0,2,1:T(8,128)}, f32[16,3,2,1024]{3,0,2,1:T(8,128)S(1)}, u32[]{:S(2)}) copy-start(f32[16,3,2,1024]{3,0,2,1:T(8,128)S(1)} %convolution_subtract_fusion.3) | copy-start | bytes 1179652
  93.6 37.8 %copy-start.6 = (f32[16,3,2,1024]{3,0,2,1:T(8,128)}, f32[16,3,2,1024]{3,0,2,1:T(8,128)S(1)}, u32[]{:S(2)}) copy-start(f32[16,3,2,1024]{3,0,2,1:T(8,128)S(1)} %convolution_add_fusion.3) | copy-start | bytes 1179652
  180.2 6.2 %copy-start = (f32[1,3,2,16384]{3,2,1,0:T(2,128)S(1)}, f32[1,3,2,16384]{3,2,1,0:T(2,128)}, u32[]{:S(2)}) copy-start(f32[1,3,2,16384]{3,2,1,0:T(2,128)} %stack_reshape.4) | copy-start | bytes 1179652
  180.2 6.2 %copy-start.1 = (f32[1,3,2,16384]{3,2,1,0:T(2,128)S(1)}, f32[1,3,2,16384]{3,2,1,0:T(2,128)}, u32[]{:S(2)}) copy-start(f32[1,3,2,16384]{3,2,1,0:T(2,128)} %stack_reshape.5) | copy-start | bytes 1179652
  180.2 6.3 %copy-start.15 = (s32[2]{0:T(128)S(1)}, s32[2]{0:T(128)}, u32[]{:S(2)}) copy-start(s32[2]{0:T(128)} %get-tuple-element.47) | copy-start | bytes 28
  180.2 6.3 %copy-start.18 = (s32[2]{0:T(128)S(1)}, s32[2]{0:T(128)}, u32[]{:S(2)}) copy-start(s32[2]{0:T(128)} %get-tuple-element.46) | copy-start | bytes 28
  184.8 4.4 copy-start.4
  218.9 0.8 copy-start.13
  219.8 18.7 %copy-start.19 = (f32[5,2,16,1024]{3,2,1,0:T(8,128)S(1)}, f32[5,2,16,1024]{3,2,1,0:T(8,128)}, u32[]{:S(2)}) copy-start(f32[5,2,16,1024]{3,2,1,0:T(8,128)} %fusion.16) | copy-start | bytes 1966084
  238.5 20.3 %copy-start.12 = (f32[5,2,1024,16]{2,3,1,0:T(8,128)S(1)}, f32[5,2,1024,16]{2,3,1,0:T(8,128)}, u32[]{:S(2)}) copy-start(f32[5,2,1024,16]{2,3,1,0:T(8,128)} %constant_dynamic-update-slice_fusion) | copy-start | bytes 1966084
  303.2 34.8 %all-to-all-start.4 = ((f32[2,5,4,1,2,1,4,1024]{7,2,4,1,0,5,3,6:T(4,128)}), f32[2,5,4,1,2,1,4,1024]{7,2,4,1,0,5,3,6:T(4,128)S(1)}, u32[]{:S(2)}, u32[]{:S(2)}) async-start(f32[2,5,4,1,2,1,4,1024]{7,2,4,1,0,5,3,6:T(4,128)} %copy.110), calls=%async_computation.4 | async-start | bytes 2621440 | tf_op jit(solution)/shard_map/all_to_all | solution.py:162
  350.8 25.3 %copy-start.9 = (f32[16,1024]{1,0:T(8,128)S(1)}, f32[16,1024]{1,0:T(8,128)}, u32[]{:S(2)}) copy-start(f32[16,1024]{1,0:T(8,128)} %copy-done.8) | copy-start | bytes 196612
  350.8 25.3 %copy-start.11 = (f32[16,1024]{1,0:T(8,128)S(1)}, f32[16,1024]{1,0:T(8,128)}, u32[]{:S(2)}) copy-start(f32[16,1024]{1,0:T(8,128)} %copy-done.10) | copy-start | bytes 196612
  362.3 12.2 %all-to-all-start.6 = ((f32[2,1,1,4,2,4,1,1024]{7,4,5,0,6,2,1,3:T(2,128)}), f32[2,1,1,4,2,4,1,1024]{7,4,5,0,6,2,1,3:T(2,128)S(1)}, u32[]{:S(2)}, u32[]{:S(2)}) async-start(f32[2,1,1,4,2,4,1,1024]{7,4,5,0,6,2,1,3:T(2,128)} %copy.130), calls=%async_computation.6 | async-start | bytes 524288 | tf_op jit(solution)/shard_map/all_to_all | solution.py:146
  432.0 19.2 %copy-start.3 = (s32[16384]{0:T(1024)S(1)}, s32[16384]{0:T(1024)}, u32[]{:S(2)}) copy-start(s32[16384]{0:T(1024)} %copy-done.2) | copy-start | bytes 196612
  432.1 19.2 %copy-start.7 = (f32[2,16384]{1,0:T(2,128)S(1)}, f32[2,16384]{1,0:T(2,128)}, u32[]{:S(2)}) copy-start(f32[2,16384]{1,0:T(2,128)} %param.9) | copy-start | bytes 393220
  432.1 19.1 %copy-start.16 = (s32[2]{0:T(128)S(1)}, s32[2]{0:T(128)}, u32[]{:S(2)}) copy-start(s32[2]{0:T(128)} %get-tuple-element.47) | copy-start | bytes 28
  432.1 19.1 %copy-start.17 = (f32[2]{0:T(128)S(1)}, f32[2]{0:T(128)}, u32[]{:S(2)}) copy-start(f32[2]{0:T(128)} %get-tuple-element.45) | copy-start | bytes 28
where the time goes:
time: 579 us; the launch traced here: 572 us
  matrix products  342 us (59%)
  blocking collectives  70.2 us (12%)
  local copies, waits for them, and re-layouts  64.4 us (11%)
  waiting for transfers between devices  56.5 us (10%)
  starting transfers between devices  17.1 us (3%)
  other arithmetic  12.7 us (2%)
  between operations  8.9 us (2%)
    dot_general x16, matrix products, complex_einsum(): imag_out = jnp.einsum(formula, data_real, table_imag, precision=exact_mode)  86.3 us
    dot_general x15, matrix products, complex_einsum(): jnp.einsum(formula, data_imag, table_imag, precision=exact_mode)  86.3 us
    dot_general x16, matrix products, complex_einsum(): real_out = jnp.einsum(formula, data_real, table_real, precision=exact_mode)  85.9 us
    dot_general x15, matrix products, complex_einsum(): jnp.einsum(formula, data_imag, table_real, precision=exact_mode)  83.7 us
    all_to_all x1, waiting for transfers between devices, to_space(): lax.all_to_all(lax.all_to_all(shaped, 'rows', split_axis=5, concat_axis=2...  31 us
    all_to_all x2, blocking collectives, to_space(): lax.all_to_all(shaped, 'rows', split_axis=5, concat_axis=2, tiled=True)  28.1 us
    unnamed x51, local copies, waits for them, and re-layouts  26.6 us
    all_to_all x2, blocking collectives, to_frequency(): lax.all_to_all(shaped, 'rows', split_axis=2, concat_axis=5, tiled=True)  22.4 us
  transfers between devices with their start and end apart: 4, of which 4 were waited for; matrix products, arithmetic and copies ran while one was open for 1% of the time, Pallas kernels for 0%

commit v1 on v0

--- a/solution.py
+++ b/solution.py
@@ -6,6 +6,30 @@
 
 NC = 16384
 exact_mode = lax.Precision.HIGHEST
+
+
+def in_blocks(array, dim, size):
+    lengths = array.shape
+    tiles = array.reshape(*lengths[:dim], size, lengths[dim] // size, *lengths[dim + 1 :])
+    return jnp.moveaxis(tiles, dim, 0)
+
+
+def laid_out(blocks, dim):
+    shape = list(blocks.shape[1:])
+    shape[dim] *= blocks.shape[0]
+    return jnp.moveaxis(blocks, 0, dim).reshape(shape)
+
+
+def rotated_exchange(x, axis, split_dim, concat_dim):
+    devices, here = (lax.axis_size(axis), lax.axis_index(axis))
+    blocks = in_blocks(x, split_dim, devices)
+    out = blocks
+    for step in range(1, devices):
+        target, source = ((here + step) % devices, (here - step) % devices)
+        sent = lax.dynamic_index_in_dim(blocks, target, 0)
+        received = lax.ppermute(sent, axis, [(i, (i + step) % devices) for i in range(devices)])
+        out = lax.dynamic_update_slice_in_dim(out, received, source, axis=0)
+    return laid_out(out, concat_dim)
 
 
 def split_factor(length):
@@ -143,12 +167,8 @@
         shaped = stacked.reshape(
             2, batch_len, rows_count, fields_count, local_rows, 1, 1, block_width
         )
-        arrived = lax.all_to_all(
-            lax.all_to_all(shaped, "rows", split_axis=2, concat_axis=5, tiled=True),
-            "fields",
-            split_axis=3,
-            concat_axis=6,
-            tiled=True,
+        arrived = rotated_exchange(
+            lax.all_to_all(shaped, "rows", split_axis=2, concat_axis=5, tiled=True), "fields", 3, 6
         )
         result = forward_columns(arrived.reshape(2, batch_len, local_rows, groups * block_width))
         return result

time: 579 us -> 574 us (level)
  blocking collectives: 70.2 us -> 57.9 us
  starting transfers between devices: 17.1 us -> 25.2 us
    all_to_all x2 -> x1, blocking collectives: 22.4 us -> 8.39 us  [to_frequency(): lax.all_to_all(shaped, 'rows', split_axis=2, concat_axis=5, tiled=True)]
    ppermute x0 -> x6, waiting for transfers between devices: none -> 13.6 us  [rotated_exchange(): lax.ppermute(sent, axis, [(i, (i + step) % devices) for i in range(device...]
    all_to_all x2 -> x1, waiting for transfers between devices: 18.2 us -> 5.61 us  [to_frequency(): lax.all_to_all(shaped, 'rows', split_axis=2, concat_axis=5, tiled=True)]
    ppermute x0 -> x6, starting transfers between devices: none -> 10.2 us  [rotated_exchange(): lax.ppermute(sent, axis, [(i, (i + step) % devices) for i in range(device...]
  transfers between devices with their start and end apart: 4 -> 9, of which waited for: 4 -> 7; matrix products, arithmetic and copies ran while one was open for 1% -> 1% of each run, Pallas kernels for 0% -> 0%
where the time goes in v1:
time: 574 us; the launch traced here: 566 us
  matrix products  342 us (60%)
  local copies, waits for them, and re-layouts  63.3 us (11%)
  blocking collectives  57.9 us (10%)
  waiting for transfers between devices  55.8 us (10%)
  starting transfers between devices  25.2 us (4%)
  other arithmetic  12.8 us (2%)
  between operations  8.93 us (2%)
    dot_general x16, matrix products, complex_einsum(): real_out = jnp.einsum(formula, data_real, table_real, precision=exact_mode)  86.7 us
    dot_general x16, matrix products, complex_einsum(): imag_out = jnp.einsum(formula, data_real, table_imag, precision=exact_mode)  86.5 us
    dot_general x15, matrix products, complex_einsum(): jnp.einsum(formula, data_imag, table_imag, precision=exact_mode)  85.7 us
    dot_general x15, matrix products, complex_einsum(): jnp.einsum(formula, data_imag, table_real, precision=exact_mode)  83.5 us
    all_to_all x1, waiting for transfers between devices, to_space(): lax.all_to_all(lax.all_to_all(shaped, 'rows', split_axis=5, concat_axis=2...  30.7 us
    all_to_all x2, blocking collectives, to_space(): lax.all_to_all(shaped, 'rows', split_axis=5, concat_axis=2, tiled=True)  28.1 us
    unnamed x51, local copies, waits for them, and re-layouts  26.6 us
    ppermute x6, waiting for transfers between devices, rotated_exchange(): lax.ppermute(sent, axis, [(i, (i + step) % devices) for i in range(device...  13.6 us
  transfers between devices with their start and end apart: 9, of which 7 were waited for; matrix products, arithmetic and copies ran while one was open for 1% of the time, Pallas kernels for 0%

profile of v1, /device:TPU:0, one launch (start us, length us, event | category | flops | bytes accessed | tf_op | source)
XLA Modules:
  0.0 566.3 jit_solution(219127687024121948)
XLA Ops:
  0.0 6.7 %copy.84 = f32[3,8,4096]{1,0,2:T(4,128)} copy(f32[3,8,4096]{2,1,0:T(8,128)} %param.5) | data formatting | bytes 786432 | tf_op args[0]
  6.7 7.5 %reshape.1882 = f32[4,1,24576]{2,1,0:T(1,128)} reshape(f32[4096,3,8]{2,1,0:T(4,128)} %bitcast.483) | data formatting | bytes 786432
  14.2 4.3 all-to-all-start
  20.1 5.8 %all-to-all-done = f32[4,1,24576]{2,1,0:T(1,128)S(1)} async-done(((f32[4,1,24576]{2,1,0:T(1,128)}), f32[4,1,24576]{2,1,0:T(1,128)S(1)}, u32[]{:S(2)}, u32[]{:S(2)}) %all-to-all-start) | async-done | bytes 393248 | tf_op jit(solution)/shard_map/all_to_all | solution.py:194
  26.4 1.8 reduce
  28.2 8.8 %reshape.1883 = f32[4096,3,8]{2,1,0:T(4,128)} reshape(f32[4,24576]{1,0:T(4,128)S(1)} %reduce) | data formatting | bytes 786432
  36.9 6.7 %copy.168 = f32[3,8,4,1024]{3,2,1,0:T(4,128)S(1)} copy(f32[3,8,4,1024]{1,0,3,2:T(4,128)} %bitcast.482) | data formatting | bytes 786432 | tf_op jit(solution)/shard_map/all_to_all | solution.py:194
  43.6 0.8 fusion.133
  44.5 0.9 add_bitcast_fusion.1
  49.8 1.0 copy.92
  50.8 3.5 all-to-all-start.1
  60.3 5.6 all-to-all-done.1
  65.9 2.3 collective-permute-start
  68.2 2.6 collective-permute-start.1
  71.3 1.3 collective-permute-start.2
  72.7 3.4 collective-permute-done
  76.1 7.2 %collective-permute-done.1 = f32[1,2,3,1,1,2,4,1,1024]{8,5,0,2,1,6,7,4,3:T(2,128)S(1)} collective-permute-done((f32[1,2,3,1,1,2,4,1,1024]{8,5,0,2,1,6,7,4,3:T(2,128)S(1)}, f32[1,2,3,1,1,2,4,1,1024]{8,5,0,2,1,6,7,4,3:T(2,128)S(1)}, u32[]{:S(2)}, u32[]{:S(2)}) %collective-permute-start.1) | collective-permute-done | bytes 196640 | tf_op jit(solution)/shard_map/ppermute | solution.py:30
  86.2 19.1 %fusion.24 = f32[1024,3,2,16]{0,3,2,1:T(8,128)S(1)} fusion(f32[16,3,2,1024]{3,0,2,1:T(8,128)S(1)} %convolution_add_fusion.3, f32[16,3,2,1024]{3,0,2,1:T(8,128)S(1)} %convolution_subtract_fusion.3, f32[16,1024]{1,0:T(8,128)S(1)} %get-tuple-element.58, f32[16,1024]{1,0:T(8,128)S(1)} %get-tuple-element.59), kind=kOutput, calls=%fused_computation.27 | convolution fusion | flops 1222934528 | bytes 1310720 | tf_op jit(solution)/shard_map/brkc,cq->brqk/dot_general | solution.py:52
  105.3 19.0 %fusion.22 = f32[1024,3,2,16]{0,3,2,1:T(8,128)} fusion(f32[16,3,2,1024]{3,0,2,1:T(8,128)S(1)} %convolution_add_fusion.3, f32[16,3,2,1024]{3,0,2,1:T(8,128)S(1)} %convolution_subtract_fusion.3, f32[16,1024]{1,0:T(8,128)S(1)} %get-tuple-element.58, f32[16,1024]{1,0:T(8,128)S(1)} %get-tuple-element.59), kind=kOutput, calls=%fused_computation.25 | convolution fusion | flops 1222934528 | bytes 1310720 | tf_op jit(solution)/shard_map/brkc,cq->brqk/dot_general | solution.py:56
  124.4 19.4 %fusion.88 = f32[3,2,1024,16]{2,3,1,0:T(8,128)} fusion(f32[1024,3,2,16]{0,3,2,1:T(8,128)S(1)} %fusion.24, f32[16,3,2,1024]{3,0,2,1:T(8,128)S(1)} %convolution_add_fusion.3, f32[16,3,2,1024]{3,0,2,1:T(8,128)S(1)} %convolution_subtract_fusion.3, f32[16,1024]{1,0:T(8,128)S(1)} %get-tuple-element.58, f32[16,1024]{1,0:T(8,128)S(1)} %get-tuple-element.59), kind=kOutput, calls=%fused_computation.84 | convolution fusion | flops 1223032832 | bytes 1703936 | tf_op jit(solution)/shard_map/brkc,cq->brqk/dot_general | solution.py:55
  143.8 1.9 copy.95
  145.7 2.4 stack_reshape.4
  148.1 20.5 %fusion.94 = f32[3,2,1024,16]{2,3,1,0:T(8,128)} fusion(f32[1024,3,2,16]{0,3,2,1:T(8,128)} %fusion.22, f32[16,3,2,1024]{3,0,2,1:T(8,128)} %copy-done.6, f32[16,3,2,1024]{3,0,2,1:T(8,128)} %copy-done.5, f32[16,1024]{1,0:T(8,128)} %copy-done.8, f32[16,1024]{1,0:T(8,128)} %copy-done.10), kind=kOutput, calls=%fused_computation.86 | convolution fusion | flops 1223032832 | bytes 1703936 | tf_op jit(solution)/shard_map/brkc,cq->brqk/dot_general | solution.py:53
  168.6 2.1 copy.96
  170.7 2.5 stack_reshape.5
  173.2 2.9 fusion.150
  176.1 1.3 fusion.152
  179.4 1.5 subtract_negate_fusion.1
  182.1 1.3 fusion.153
  184.1 1.3 stack.74
  188.4 20.5 %fusion.16 = f32[5,2,16,1024]{3,2,1,0:T(8,128)} fusion(f32[5,2,1024,16]{2,3,1,0:T(8,128)} %constant_dynamic-update-slice_fusion), kind=kOutput, calls=%fused_computation.19 | convolution fusion | flops 2027945984 | bytes 1310720 | tf_op jit(solution)/shard_map/brqk,qc->brkc/dot_general | solution.py:52
  212.1 0.8 copy-done.13
  213.0 18.7 %fusion.14 = f32[5,2,16,1024]{3,2,1,0:T(8,128)S(1)} fusion(f32[5,2,1024,16]{2,3,1,0:T(8,128)S(1)} %constant_dynamic-update-slice_fusion.5), kind=kOutput, calls=%fused_computation.17 | convolution fusion | flops 2027945984 | bytes 1310720 | tf_op jit(solution)/shard_map/brqk,qc->brkc/dot_general | solution.py:56
  231.7 19.9 %fusion.77 = f32[5,2,16,1024]{3,2,1,0:T(8,128)S(1)} fusion(f32[5,2,16,1024]{3,2,1,0:T(8,128)S(1)} %copy-done.19, f32[5,2,1024,16]{2,3,1,0:T(8,128)} %copy-done.13), kind=kOutput, calls=%fused_computation.75 | convolution fusion | flops 2028109824 | bytes 1966080 | tf_op jit(solution)/shard_map/brqk,qc->brkc/dot_general | solution.py:55
  251.6 18.9 %fusion.80 = f32[5,2,16,1024]{3,2,1,0:T(8,128)S(1)} fusion(f32[5,2,16,1024]{3,2,1,0:T(8,128)S(1)} %fusion.14, f32[5,2,1024,16]{2,3,1,0:T(8,128)S(1)} %copy-done.12), kind=kOutput, calls=%fused_computation.76 | convolution fusion | flops 2028109824 | bytes 1966080 | tf_op jit(solution)/shard_map/brqk,qc->brkc/dot_general | solution.py:53
  273.1 0.8 fusion.72
  274.6 19.7 %all_to_all.129 = f32[2,5,1,1,2,4,4,1024]{7,6,4,1,3,2,0,5:T(4,128)S(1)} all-to-all(f32[2,5,1,1,2,4,4,1024]{7,6,4,1,3,2,0,5:T(4,128)S(1)} %copy.169), channel_id=1, replica_groups=mesh['sims'=2,'rows'=4,'fields'=4] {'rows'}, dimensions={5} | all-to-all | bytes 2621440 | tf_op jit(solution)/shard_map/all_to_all | solution.py:183
  294.3 1.9 copy.109
  296.2 7.2 %all-to-all-start.3 = ((f32[2,5,4,1,2,1,4,1024]{7,2,4,1,0,5,3,6:T(4,128)}), f32[2,5,4,1,2,1,4,1024]{7,2,4,1,0,5,3,6:T(4,128)S(1)}, u32[]{:S(2)}, u32[]{:S(2)}) async-start(f32[2,5,4,1,2,1,4,1024]{7,2,4,1,0,5,3,6:T(4,128)} %copy.109), calls=%async_computation.3 | async-start | bytes 2621440 | tf_op jit(solution)/shard_map/all_to_all | solution.py:182
  303.5 30.7 %all-to-all-done.3 = f32[2,5,4,1,2,1,4,1024]{7,2,4,1,0,5,3,6:T(4,128)S(1)} async-done(((f32[2,5,4,1,2,1,4,1024]{7,2,4,1,0,5,3,6:T(4,128)}), f32[2,5,4,1,2,1,4,1024]{7,2,4,1,0,5,3,6:T(4,128)S(1)}, u32[]{:S(2)}, u32[]{:S(2)}) %all-to-all-start.3) | async-done | bytes 1310752 | tf_op jit(solution)/shard_map/all_to_all | solution.py:182
  334.4 1.2 fusion.318
  335.7 1.2 fusion.316
  337.0 1.3 convolution_add_fusion.2
  338.2 1.5 add_bitcast_fusion
  339.8 1.0 fusion.127
  340.8 1.0 fusion.125
  341.8 1.0 fusion.74
  343.5 1.0 fusion.76
  345.8 0.9 fusion.185
  349.5 8.4 %all_to_all.130 = f32[2,1,4,4,2,1,1,1024]{7,4,3,6,5,1,0,2:T(2,128)S(1)} all-to-all(f32[2,1,4,4,2,1,1,1024]{7,4,3,6,5,1,0,2:T(2,128)S(1)} %copy.128), channel_id=1, replica_groups=mesh['sims'=2,'rows'=4,'fields'=4] {'rows'}, dimensions={2} | all-to-all | bytes 524288 | tf_op jit(solution)/shard_map/all_to_all | solution.py:171
  360.3 2.1 collective-permute-start.4
  362.4 1.9 collective-permute-start.5
  364.3 2.8 collective-permute-done.4
  368.6 18.3 %fusion.12 = f32[1024,2,16]{0,2,1:T(8,128)S(1)} fusion(f32[16,1,2,1024]{3,0,2,1:T(8,128)S(1)} %fusion.97, f32[16,1,2,1024]{3,0,2,1:T(8,128)S(1)} %fusion.98, f32[16,1024]{1,0:T(8,128)S(1)} %copy-done.9, f32[16,1024]{1,0:T(8,128)S(1)} %copy-done.11), kind=kOutput, calls=%fused_computation.15 | convolution fusion | flops 417431552 | bytes 524288 | tf_op jit(solution)/shard_map/brkc,cq->brqk/dot_general | solution.py:55
  387.0 18.3 %fusion.10 = f32[1024,2,16]{0,2,1:T(8,128)S(1)} fusion(f32[16,1,2,1024]{3,0,2,1:T(8,128)S(1)} %fusion.97, f32[16,1,2,1024]{3,0,2,1:T(8,128)S(1)} %fusion.98, f32[16,1024]{1,0:T(8,128)S(1)} %copy-done.9, f32[16,1024]{1,0:T(8,128)S(1)} %copy-done.11), kind=kOutput, calls=%fused_computation.13 | convolution fusion | flops 417431552 | bytes 524288 | tf_op jit(solution)/shard_map/brkc,cq->brqk/dot_general | solution.py:53
  405.3 18.4 %fusion.114 = f32[1,2,1024,16]{2,3,1,0:T(8,128)S(1)} fusion(f32[1024,2,16]{0,2,1:T(8,128)S(1)} %fusion.12, f32[16,1,2,1024]{3,0,2,1:T(8,128)S(1)} %fusion.97, f32[16,1,2,1024]{3,0,2,1:T(8,128)S(1)} %fusion.98, f32[16,1024]{1,0:T(8,128)S(1)} %copy-done.9, f32[16,1024]{1,0:T(8,128)S(1)} %copy-done.11), kind=kOutput, calls=%fused_computation.110 | convolution fusion | flops 417464320 | bytes 655360 | tf_op jit(solution)/shard_map/brkc,cq->brqk/dot_general | solution.py:52
  424.6 18.2 %fusion.120 = f32[1,2,1024,16]{2,3,1,0:T(8,128)S(1)} fusion(f32[1024,2,16]{0,2,1:T(8,128)S(1)} %fusion.10, f32[16,1,2,1024]{3,0,2,1:T(8,128)S(1)} %fusion.97, f32[16,1,2,1024]{3,0,2,1:T(8,128)S(1)} %fusion.98, f32[16,1024]{1,0:T(8,128)S(1)} %copy-done.9, f32[16,1024]{1,0:T(8,128)S(1)} %copy-done.11), kind=kOutput, calls=%fused_computation.112 | convolution fusion | flops 417464320 | bytes 655360 | tf_op jit(solution)/shard_map/brkc,cq->brqk/dot_general | solution.py:56
  444.5 21.4 %fusion.4 = f32[2,16,1024]{2,1,0:T(8,128)S(1)} fusion(f32[2,1024,16]{2,1,0:T(8,128)S(1)} %reshape.1845), kind=kOutput, calls=%fused_computation.7 | convolution fusion | flops 417333248 | bytes 262144 | tf_op jit(solution)/shard_map/brqk,qc->brkc/dot_general | solution.py:55
  466.3 21.2 %fusion.2 = f32[2,16,1024]{2,1,0:T(8,128)S(1)} fusion(f32[2,1024,16]{2,1,0:T(8,128)S(1)} %reshape.1844), kind=kOutput, calls=%fused_computation.5 | convolution fusion | flops 417333248 | bytes 262144 | tf_op jit(solution)/shard_map/brqk,qc->brkc/dot_general | solution.py:53
  487.5 21.5 %fusion.105 = f32[2,16,1024]{2,1,0:T(8,128)S(1)} fusion(f32[2,16,1024]{2,1,0:T(8,128)S(1)} %fusion.4, f32[2,1024,16]{2,1,0:T(8,128)S(1)} %reshape.1844), kind=kOutput, calls=%fused_computation.107 | convolution fusion | flops 417366016 | bytes 393216 | tf_op jit(solution)/shard_map/brqk,qc->brkc/dot_general | solution.py:52
  508.9 21.1 %fusion.108 = f32[2,16,1024]{2,1,0:T(8,128)S(1)} fusion(f32[2,16,1024]{2,1,0:T(8,128)S(1)} %fusion.2, f32[2,1024,16]{2,1,0:T(8,128)S(1)} %reshape.1845), kind=kOutput, calls=%fused_computation.108 | convolution fusion | flops 417366016 | bytes 393216 | tf_op jit(solution)/shard_map/brqk,qc->brkc/dot_general | solution.py:56
  531.7 8.4 %all_to_all.131 = f32[2,1,1,1,2,4,4,1024]{7,6,4,3,2,1,0,5:T(4,128)S(1)} all-to-all(f32[2,1,1,1,2,4,4,1024]{7,6,4,3,2,1,0,5:T(4,128)S(1)} %copy.172), channel_id=1, replica_groups=mesh['sims'=2,'rows'=4,'fields'=4] {'rows'}, dimensions={5} | all-to-all | bytes 524288 | tf_op jit(solution)/shard_map/all_to_all | solution.py:183
  540.3 13.1 %all_to_all.132 = f32[2,1,4,1,2,1,4,1024]{7,2,4,0,5,3,1,6:T(4,128)S(1)} all-to-all(f32[2,1,4,1,2,1,4,1024]{7,2,4,0,5,3,1,6:T(4,128)S(1)} %copy.139), channel_id=1, replica_groups=mesh['sims'=2,'rows'=4,'fields'=4] {'fields'}, dimensions={6} | all-to-all | bytes 524288 | tf_op jit(solution)/shard_map/all_to_all | solution.py:182
  557.0 8.4 %all_to_all.133 = f32[2,32,1024]{2,0,1:T(2,128)S(1)} all-to-all(f32[2,32,1024]{2,0,1:T(2,128)S(1)} %copy.146), channel_id=1, replica_groups=mesh['sims'=2,'rows'=4,'fields'=4] {'rows'}, dimensions={1} | all-to-all | bytes 524288 | tf_op jit(solution)/shard_map/all_to_all | solution.py:274
  (176 shorter events, 39.4 us)
Async XLA Ops:
  6.7 12.4 %copy-start.14 = (s32[6]{0:T(128)S(1)}, s32[6]{0:T(128)}, u32[]{:S(2)}) copy-start(s32[6]{0:T(128)} %param.6) | copy-start | bytes 76
  14.2 11.7 %all-to-all-start = ((f32[4,1,24576]{2,1,0:T(1,128)}), f32[4,1,24576]{2,1,0:T(1,128)S(1)}, u32[]{:S(2)}, u32[]{:S(2)}) async-start(f32[4,1,24576]{2,1,0:T(1,128)} %reshape.1882), calls=%async_computation | async-start | bytes 786432 | tf_op jit(solution)/shard_map/all_to_all | solution.py:194
  20.1 104.3 %copy-start.8 = (f32[16,1024]{1,0:T(8,128)}, f32[16,1024]{1,0:T(8,128)S(1)}, u32[]{:S(2)}) copy-start(f32[16,1024]{1,0:T(8,128)S(1)} %get-tuple-element.58) | copy-start | bytes 196612
  20.1 104.3 %copy-start.10 = (f32[16,1024]{1,0:T(8,128)}, f32[16,1024]{1,0:T(8,128)S(1)}, u32[]{:S(2)}) copy-start(f32[16,1024]{1,0:T(8,128)S(1)} %get-tuple-element.59) | copy-start | bytes 196612
  50.8 15.1 %all-to-all-start.1 = ((f32[2,3,4,4,2,1,1,1024]{7,4,3,1,6,5,0,2:T(2,128)}), f32[2,3,4,4,2,1,1,1024]{7,4,3,1,6,5,0,2:T(2,128)S(1)}, u32[]{:S(2)}, u32[]{:S(2)}) async-start(f32[2,3,4,4,2,1,1,1024]{7,4,3,1,6,5,0,2:T(2,128)} %copy.92), calls=%async_computation.1 | async-start | bytes 1572864 | tf_op jit(solution)/shard_map/all_to_all | solution.py:171
  60.3 119.1 %copy-start.2 = (s32[16384]{0:T(1024)}, s32[16384]{0:T(1024)S(1)}, u32[]{:S(2)}) copy-start(s32[16384]{0:T(1024)S(1)} %get-tuple-element.62) | copy-start | bytes 196612
  65.9 10.2 %collective-permute-start = (f32[1,2,3,1,1,2,4,1,1024]{8,5,0,2,1,6,7,4,3:T(2,128)S(1)}, f32[1,2,3,1,1,2,4,1,1024]{8,5,0,2,1,6,7,4,3:T(2,128)S(1)}, u32[]{:S(2)}, u32[]{:S(2)}) collective-permute-start(f32[1,2,3,1,1,2,4,1,1024]{8,5,0,2,1,6,7,4,3:T(2,128)S(1)} %get-tuple-element.25), channel_id=1, source_target_pairs={{0,1},{1,2},{2,3},{3,0},{4,5},{5,6},{6,7},{7,4},{8,9},{9,10},{10,1... | collective-permute-start | bytes 589832 | tf_op jit(solution)/shard_map/ppermute | solution.py:30
  68.2 15.1 %collective-permute-start.1 = (f32[1,2,3,1,1,2,4,1,1024]{8,5,0,2,1,6,7,4,3:T(2,128)S(1)}, f32[1,2,3,1,1,2,4,1,1024]{8,5,0,2,1,6,7,4,3:T(2,128)S(1)}, u32[]{:S(2)}, u32[]{:S(2)}) collective-permute-start(f32[1,2,3,1,1,2,4,1,1024]{8,5,0,2,1,6,7,4,3:T(2,128)S(1)} %get-tuple-element.24), channel_id=1, source_target_pairs={{0,2},{1,3},{2,0},{3,1},{4,6},{5,7},{6,4},{7,5},{8,10},{9,11},{10,... | collective-permute-start | bytes 589832 | tf_op jit(solution)/shard_map/ppermute | solution.py:30
  71.3 12.1 %collective-permute-start.2 = (f32[1,2,3,1,1,2,4,1,1024]{8,5,0,2,1,6,7,4,3:T(2,128)S(1)}, f32[1,2,3,1,1,2,4,1,1024]{8,5,0,2,1,6,7,4,3:T(2,128)S(1)}, u32[]{:S(2)}, u32[]{:S(2)}) collective-permute-start(f32[1,2,3,1,1,2,4,1,1024]{8,5,0,2,1,6,7,4,3:T(2,128)S(1)} %get-tuple-element.23), channel_id=1, source_target_pairs={{0,3},{1,0},{2,1},{3,2},{4,7},{5,4},{6,5},{7,6},{8,11},{9,8},{10,9... | collective-permute-start | bytes 589832 | tf_op jit(solution)/shard_map/ppermute | solution.py:30
  85.7 38.7 %copy-start.5 = (f32[16,3,2,1024]{3,0,2,1:T(8,128)}, f32[16,3,2,1024]{3,0,2,1:T(8,128)S(1)}, u32[]{:S(2)}) copy-start(f32[16,3,2,1024]{3,0,2,1:T(8,128)S(1)} %convolution_subtract_fusion.3) | copy-start | bytes 1179652
  86.2 38.2 %copy-start.6 = (f32[16,3,2,1024]{3,0,2,1:T(8,128)}, f32[16,3,2,1024]{3,0,2,1:T(8,128)S(1)}, u32[]{:S(2)}) copy-start(f32[16,3,2,1024]{3,0,2,1:T(8,128)S(1)} %convolution_add_fusion.3) | copy-start | bytes 1179652
  173.2 6.2 %copy-start = (f32[1,3,2,16384]{3,2,1,0:T(2,128)S(1)}, f32[1,3,2,16384]{3,2,1,0:T(2,128)}, u32[]{:S(2)}) copy-start(f32[1,3,2,16384]{3,2,1,0:T(2,128)} %stack_reshape.4) | copy-start | bytes 1179652
  173.2 6.3 %copy-start.1 = (f32[1,3,2,16384]{3,2,1,0:T(2,128)S(1)}, f32[1,3,2,16384]{3,2,1,0:T(2,128)}, u32[]{:S(2)}) copy-start(f32[1,3,2,16384]{3,2,1,0:T(2,128)} %stack_reshape.5) | copy-start | bytes 1179652
  173.2 6.3 %copy-start.15 = (s32[2]{0:T(128)S(1)}, s32[2]{0:T(128)}, u32[]{:S(2)}) copy-start(s32[2]{0:T(128)} %get-tuple-element.57) | copy-start | bytes 28
  173.2 6.3 %copy-start.18 = (s32[2]{0:T(128)S(1)}, s32[2]{0:T(128)}, u32[]{:S(2)}) copy-start(s32[2]{0:T(128)} %get-tuple-element.56) | copy-start | bytes 28
  177.7 4.4 copy-start.4
  212.1 0.9 copy-start.13
  213.0 18.7 %copy-start.19 = (f32[5,2,16,1024]{3,2,1,0:T(8,128)S(1)}, f32[5,2,16,1024]{3,2,1,0:T(8,128)}, u32[]{:S(2)}) copy-start(f32[5,2,16,1024]{3,2,1,0:T(8,128)} %fusion.16) | copy-start | bytes 1966084
  231.7 19.9 %copy-start.12 = (f32[5,2,1024,16]{2,3,1,0:T(8,128)S(1)}, f32[5,2,1024,16]{2,3,1,0:T(8,128)}, u32[]{:S(2)}) copy-start(f32[5,2,1024,16]{2,3,1,0:T(8,128)} %constant_dynamic-update-slice_fusion) | copy-start | bytes 1966084
  296.2 38.0 %all-to-all-start.3 = ((f32[2,5,4,1,2,1,4,1024]{7,2,4,1,0,5,3,6:T(4,128)}), f32[2,5,4,1,2,1,4,1024]{7,2,4,1,0,5,3,6:T(4,128)S(1)}, u32[]{:S(2)}, u32[]{:S(2)}) async-start(f32[2,5,4,1,2,1,4,1024]{7,2,4,1,0,5,3,6:T(4,128)} %copy.109), calls=%async_computation.3 | async-start | bytes 2621440 | tf_op jit(solution)/shard_map/all_to_all | solution.py:182
  345.3 23.3 %copy-start.9 = (f32[16,1024]{1,0:T(8,128)S(1)}, f32[16,1024]{1,0:T(8,128)}, u32[]{:S(2)}) copy-start(f32[16,1024]{1,0:T(8,128)} %copy-done.8) | copy-start | bytes 196612
  345.3 23.3 %copy-start.11 = (f32[16,1024]{1,0:T(8,128)S(1)}, f32[16,1024]{1,0:T(8,128)}, u32[]{:S(2)}) copy-start(f32[16,1024]{1,0:T(8,128)} %copy-done.10) | copy-start | bytes 196612
  357.9 6.4 %collective-permute-start.3 = (f32[1,2,1,1,1,2,4,1,1024]{8,5,0,1,6,7,4,3,2:T(2,128)S(1)}, f32[1,2,1,1,1,2,4,1,1024]{8,5,0,1,6,7,4,3,2:T(2,128)S(1)}, u32[]{:S(2)}, u32[]{:S(2)}) collective-permute-start(f32[1,2,1,1,1,2,4,1,1024]{8,5,0,1,6,7,4,3,2:T(2,128)S(1)} %get-tuple-element.42), channel_id=1, source_target_pairs={{0,1},{1,2},{2,3},{3,0},{4,5},{5,6},{6,7},{7,4},{8,9},{9,10},{10,1... | collective-permute-start | bytes 196616 | tf_op jit(solution)/shard_map/ppermute | solution.py:30
  360.3 6.7 %collective-permute-start.4 = (f32[1,2,1,1,1,2,4,1,1024]{8,5,0,1,6,7,4,3,2:T(2,128)S(1)}, f32[1,2,1,1,1,2,4,1,1024]{8,5,0,1,6,7,4,3,2:T(2,128)S(1)}, u32[]{:S(2)}, u32[]{:S(2)}) collective-permute-start(f32[1,2,1,1,1,2,4,1,1024]{8,5,0,1,6,7,4,3,2:T(2,128)S(1)} %get-tuple-element.41), channel_id=1, source_target_pairs={{0,2},{1,3},{2,0},{3,1},{4,6},{5,7},{6,4},{7,5},{8,10},{9,11},{10,... | collective-permute-start | bytes 196616 | tf_op jit(solution)/shard_map/ppermute | solution.py:30
  362.4 4.9 collective-permute-start.5
  424.6 19.2 %copy-start.3 = (s32[16384]{0:T(1024)S(1)}, s32[16384]{0:T(1024)}, u32[]{:S(2)}) copy-start(s32[16384]{0:T(1024)} %copy-done.2) | copy-start | bytes 196612
  424.6 19.2 %copy-start.7 = (f32[2,16384]{1,0:T(2,128)S(1)}, f32[2,16384]{1,0:T(2,128)}, u32[]{:S(2)}) copy-start(f32[2,16384]{1,0:T(2,128)} %param.9) | copy-start | bytes 393220
  424.6 19.1 %copy-start.16 = (s32[2]{0:T(128)S(1)}, s32[2]{0:T(128)}, u32[]{:S(2)}) copy-start(s32[2]{0:T(128)} %get-tuple-element.57) | copy-start | bytes 28
  424.6 19.1 %copy-start.17 = (f32[2]{0:T(128)S(1)}, f32[2]{0:T(128)}, u32[]{:S(2)}) copy-start(f32[2]{0:T(128)} %get-tuple-element.55) | copy-start | bytes 28
